TPU v7x, 128 devices: a whole 4x4x4 slice. The times are simulated.
128 devices in a mesh: grp: 4 (over z), tile: 32 (over x, y, core).
Axes of the slice: x: 4, y: 4, z: 4, core: 2. Of those that a mesh axis runs over, the one named last changes fastest.
Arguments:
- noise: bfloat16 [16, 3, 2048, 2048], P('grp', None, 'tile'), may hold values from -6 to 6
- stress: float32 [6, 2048, 2048], P(None, 'tile', 'grp'), as said below
- timescale: float32 [2048, 2048], P('tile', 'grp'), may hold values from 3 to 256
- mean_inflow: float32 [2048, 2048], P('tile', 'grp'), may hold values from 0.5 to 1.5
- courant: float32 [2048, 2048], P('tile', 'grp'), may hold values from 0.2 to 0.9
- prior_state: float32 [3, 2048, 2048], P(None, 'tile', 'grp'), may hold values from -6 to 6
- field: float32 [3, 8, 2048, 2048], P(None, None, 'tile', 'grp'), may hold values from -6 to 6
Outputs:
- inflow: bfloat16 [16, 3, 2048, 2048], P(None, None, 'tile', 'grp')
- field_out: float32 [3, 8, 2048, 2048], P(None, None, 'tile', 'grp')
Inputs may be any that keep to these rules, and one draw needn't show every extreme that they name: stress holds, per cell, R11, R21, R22, R31, R32, R33 of a symmetric positive definite tensor whose Cholesky factor has diagonal entries of 0.3 or more.
All inputs are finite; a program needn't handle non-finite values.
Results may differ from a plain program's by a relative error of at most 0.0085.
Values may be sent and summed in bfloat16 or wider, within the bound.
A program may use at most 128 MiB of HBM per device.

v0:
```python
import math
import jax
import jax.numpy as jnp
from jax import lax
from jax.sharding import PartitionSpec as P

LS = 2
FW = 4


def padded_2(value, sides, width, wrap):
    for axis, dim in sides:
        devices, length = (lax.axis_size(axis), value.shape[dim])
        up = [(i, (i + 1) % devices) for i in range(devices if wrap else devices - 1)]
        down = [(j, i) for i, j in up]
        last = lax.slice_in_dim(value, length - width, length, axis=dim)
        initial = lax.slice_in_dim(value, 0, width, axis=dim)
        before = lax.ppermute(last, axis, up)
        after = lax.ppermute(initial, axis, down)
        value = jnp.concatenate([before, value, after], axis=dim)
    return value


def filter_taps():
    offsets = jnp.arange(-FW, FW + 1).astype(jnp.float32)
    raw = jnp.exp(-math.pi * offsets * offsets / (2.0 * LS * LS))
    return (raw / jnp.sqrt(jnp.sum(raw * raw))).astype(jnp.bfloat16)


def band_matrix(rows, taps):
    width = taps.shape[0]
    distance = jnp.arange(rows + width - 1)[None, :] - jnp.arange(rows)[:, None]
    picks = distance[:, :, None] == jnp.arange(width)[None, None, :]
    return jnp.sum(jnp.where(picks, taps.astype(jnp.float32), 0.0), axis=2).astype(jnp.bfloat16)


def filter_last(padded, taps):
    width = taps.shape[0]
    length = padded.shape[-1] - width + 1
    block = math.gcd(length, 128)
    weights = band_matrix(block, taps)
    windows = jnp.stack(
        [
            lax.slice_in_dim(padded, start, start + block + width - 1, axis=padded.ndim - 1)
            for start in range(0, length, block)
        ],
        axis=-2,
    )
    result = jnp.einsum("...kw,bw->...kb", windows, weights, preferred_element_type=jnp.float32)
    return result.reshape(result.shape[:-2] + (length,))


def filter_rows(padded, taps):
    rows = padded.shape[2] - taps.shape[0] + 1
    weights = band_matrix(rows, taps)
    return jnp.einsum("ij,pcjz->pciz", weights, padded, preferred_element_type=jnp.float32)


def cholesky_cells(stress):
    first_diag = jnp.sqrt(stress[0])
    second_low = stress[1] / first_diag
    second_diag = jnp.sqrt(stress[2] - second_low * second_low)
    third_low = stress[3] / first_diag
    third_mid = (stress[4] - second_low * third_low) / second_diag
    third_diag = jnp.sqrt(stress[5] - third_low * third_low - third_mid * third_mid)
    return (first_diag, second_low, second_diag, third_low, third_mid, third_diag)


def velocity_of(state, factors, mean_inflow):
    first_diag, second_low, second_diag, third_low, third_mid, third_diag = factors
    return jnp.stack(
        [
            mean_inflow + first_diag * state[0],
            second_low * state[0] + second_diag * state[1],
            third_low * state[0] + third_mid * state[1] + third_diag * state[2],
        ]
    )


def march(current, courant, velocity):
    upstream = jnp.concatenate([velocity[:, None], current[:, :-1]], axis=1)
    return (1.0 - courant) * current + courant * upstream


def tile_chain(filtered, stress, timescale, mean_inflow, courant, prior_state, field):
    decay = jnp.exp(-math.pi / (2.0 * timescale))
    gain = jnp.sqrt(1.0 - decay * decay)
    factors = cholesky_cells(stress)

    def advance(carry, plane):
        state, current = carry
        state = decay * state + gain * plane
        velocity = velocity_of(state, factors, mean_inflow)
        return ((state, march(current, courant, velocity)), velocity.astype(jnp.bfloat16))

    (state, result), inflow = lax.scan(advance, (prior_state, field), filtered)
    return (inflow, result)


def body(noise, stress, timescale, mean_inflow, courant, prior_state, field):
    taps = filter_taps()
    flipped = jnp.swapaxes(noise, 2, 3)
    tiles = lax.all_to_all(
        lax.all_to_all(flipped, "tile", split_axis=2, concat_axis=3, tiled=True),
        "grp",
        split_axis=3,
        concat_axis=0,
        tiled=True,
    )
    banded = padded_2(tiles, (("grp", 3),), FW, False)
    widened = padded_2(banded, (("tile", 2),), FW, True)
    span = filter_rows(widened, taps).astype(jnp.bfloat16)
    filtered = filter_last(span, taps)
    inflow, result = tile_chain(
        filtered, stress, timescale, mean_inflow, courant, prior_state, field
    )
    return (inflow, result)


def solution(mesh):
    placed = (
        P("grp", None, "tile", None),
        P(None, "tile", "grp"),
        P("tile", "grp"),
        P("tile", "grp"),
        P("tile", "grp"),
        P(None, "tile", "grp"),
        P(None, None, "tile", "grp"),
    )
    return jax.shard_map(
        body,
        mesh=mesh,
        in_specs=placed,
        out_specs=(P(None, None, "tile", "grp"), P(None, None, "tile", "grp")),
        check_vma=False,
    )
```

profile of v0, /device:TPU:63, one launch (start us, length us, event | category | flops | bytes accessed | tf_op | source)
XLA Modules:
  0.0 310.5 jit_solution(12647594609920412347)
XLA Ops:
  0.6 1.9 copy-done.7
  2.5 7.1 %copy.41 = bf16[4,3,64,2048]{2,0,1,3:T(4,128)(2,1)} copy(bf16[4,3,64,2048]{3,2,1,0:T(8,128)(2,1)S(1)} %copy-done.7) | data formatting | bytes 6291456 | tf_op args[0]
  9.6 7.7 %bitcast_bitcast_fusion = bf16[2048,3,4,64]{3,2,1,0:T(4,128)(2,1)} fusion(bf16[4,3,64,2048]{2,0,1,3:T(4,128)(2,1)} %copy.41), kind=kLoop, calls=%fused_computation.73 | loop fusion | bytes 6291456
  17.3 7.5 %reshape.107 = bf16[32,2,24576]{2,1,0:T(2,128)(2,1)S(1)} reshape(bf16[2048,3,4,64]{3,2,1,0:T(4,128)(2,1)} %bitcast_bitcast_fusion) | data formatting | bytes 6291456
  24.8 43.9 %all_to_all.36 = bf16[32,2,24576]{2,1,0:T(2,128)(2,1)} all-to-all(bf16[32,2,24576]{2,1,0:T(2,128)(2,1)S(1)} %reshape.107), channel_id=1, replica_groups=mesh['grp'=4,'tile'=32] {'tile'}, dimensions={0} | all-to-all | bytes 6291456 | tf_op jit(solution)/shard_map/all_to_all | solution.py:104
  68.7 8.7 %reshape.108 = bf16[2048,3,4,64]{3,2,1,0:T(4,128)(2,1)} reshape(bf16[32,2,24576]{2,1,0:T(2,128)(2,1)} %all_to_all.36) | data formatting | bytes 6291456
  77.4 9.5 %copy.65 = bf16[4,3,32,64,64]{4,2,3,1,0:T(8,128)(2,1)} copy(bf16[4,3,32,64,64]{4,0,1,3,2:T(4,128)(2,1)} %bitcast.127) | data formatting | bytes 6291456 | tf_op jit(solution)/shard_map/all_to_all | solution.py:104
  86.9 11.8 %copy.54 = bf16[4,3,64,32,64]{2,0,1,4,3:T(4,128)(2,1)} copy(bf16[4,3,64,32,64]{4,3,2,1,0:T(8,128)(2,1)} %bitcast.128) | data formatting | bytes 6291456 | tf_op jit(solution)/shard_map/all_to_all | solution.py:104
  98.7 7.7 %reshape.109 = bf16[4,2,196608]{2,1,0:T(2,128)(2,1)} reshape(bf16[2048,3,4,64]{3,2,1,0:T(4,128)(2,1)} %bitcast.129) | data formatting | bytes 6291456
  106.5 5.0 %all-to-all-start.1 = ((bf16[4,2,196608]{2,1,0:T(2,128)(2,1)}), bf16[4,2,196608]{2,1,0:T(2,128)(2,1)S(1)}, u32[]{:S(2)}, u32[]{:S(2)}) async-start(bf16[4,2,196608]{2,1,0:T(2,128)(2,1)} %reshape.109), calls=%async_computation.1 | async-start | bytes 6291456 | tf_op jit(solution)/shard_map/all_to_all | solution.py:103
  112.9 2.2 fusion.24
  115.8 1.6 fusion.26
  117.4 30.1 %all-to-all-done.1 = bf16[4,2,196608]{2,1,0:T(2,128)(2,1)S(1)} async-done(((bf16[4,2,196608]{2,1,0:T(2,128)(2,1)}), bf16[4,2,196608]{2,1,0:T(2,128)(2,1)S(1)}, u32[]{:S(2)}, u32[]{:S(2)}) %all-to-all-start.1) | async-done | bytes 3145760 | tf_op jit(solution)/shard_map/all_to_all | solution.py:103
  147.5 5.3 %reshape.110 = bf16[2048,3,4,64]{3,2,1,0:T(4,128)(2,1)} reshape(bf16[4,2,196608]{2,1,0:T(2,128)(2,1)S(1)} %all-to-all-done.1) | data formatting | bytes 6291456
  152.8 8.3 %copy.45 = bf16[4,4,3,64,512]{4,3,2,1,0:T(8,128)(2,1)S(1)} copy(bf16[4,4,3,64,512]{3,1,2,4,0:T(4,128)(2,1)} %bitcast.130) | data formatting | bytes 6291456 | tf_op jit(solution)/shard_map/all_to_all | solution.py:103
  161.1 1.5 fusion.38
  162.6 1.5 copy.46
  164.1 1.5 copy.47
  165.7 3.1 collective-permute-start.1
  168.8 2.4 collective-permute-start
  171.3 2.3 collective-permute-done
  176.1 1.8 pad_maximum_fusion.3
  177.9 5.7 %collective-permute-start.2 = (bf16[16,3,4,520]{3,2,1,0:T(4,128)(2,1)S(1)}, bf16[16,3,4,520]{3,2,1,0:T(4,128)(2,1)S(1)}, u32[]{:S(2)}, u32[]{:S(2)}) collective-permute-start(bf16[16,3,4,520]{3,2,1,0:T(4,128)(2,1)S(1)} %get-tuple-element.126), channel_id=1, source_target_pairs={{0,1},{1,2},{2,3},{3,4},{4,5},{5,6},{6,7},{7,8},{8,9},{9,10},{10,1... | collective-permute-start | bytes 599048 | tf_op jit(solution)/shard_map/ppermute | solution.py:18
  183.6 1.6 sqrt_bitcast_fusion
  185.2 1.5 collective-permute-done.2
  186.7 5.8 %collective-permute-done.3 = bf16[16,3,4,520]{3,2,1,0:T(4,128)(2,1)S(1)} collective-permute-done((bf16[16,3,4,520]{3,2,1,0:T(4,128)(2,1)S(1)}, bf16[16,3,4,520]{3,2,1,0:T(4,128)(2,1)S(1)}, u32[]{:S(2)}, u32[]{:S(2)}) %collective-permute-start.3) | collective-permute-done | bytes 199712 | tf_op jit(solution)/shard_map/ppermute | solution.py:19
  192.5 4.2 %convert_bitcast_fusion.3 = bf16[16,3,64,520]{3,2,1,0:T(8,128)(2,1)S(1)} fusion(bf16[16,3,4,520]{3,2,1,0:T(4,128)(2,1)S(1)} %collective-permute-done.3, bf16[16,3,64,4]{3,2,1,0:T(8,128)(2,1)S(1)} %copy-done.6, bf16[16,3,64,512]{3,2,1,0:T(8,128)(2,1)S(1)} %bitcast.133, bf16[16,3,64,4]{3,2,1,0:T(8,128)(2,1)S(1)} %copy-done.5, ...), kind=kOutput, calls=%fused_computation.35 | convolution fusion | flops 249600000 | bytes 6798336 | tf_op jit(solution)/shard_map/ij,pcjz->pciz/dot_general | solution.py:56
  197.6 2.6 fusion.18
  200.2 3.5 %copy.64 = f32[16,3,4,8,8,128]{5,4,2,3,1,0:T(8,128)} copy(f32[16,3,4,8,8,128]{5,4,3,2,1,0:T(8,128)S(1)} %fusion.18) | data formatting | bytes 12582912 | tf_op jit(solution)/shard_map/reshape | solution.py:50
  203.7 105.1 %while.14 = (s32[]{:T(128)}, f32[3,64,512]{2,1,0:T(8,128)S(1)}, f32[3,8,64,512]{3,2,1,0:T(8,128)S(1)}, bf16[16,3,64,512]{3,2,1,0:T(8,128)(2,1)}, f32[64,512]{1,0...) while((s32[]{:T(128)}, f32[3,64,512]{2,1,0:T(8,128)S(1)}, ...), condition=%wide.region_4.5_spmd, body=%wide.region_3.4_spmd.sunk | while | flops 4685826 | bytes 20512960 | solution.py:96
  204.6 1.3 fusion.41
  205.9 1.4 convert_bitcast_fusion.5
  208.2 1.4 fusion.42
  212.5 1.4 convert_bitcast_fusion.5
  214.7 1.4 fusion.42
  219.0 1.4 convert_bitcast_fusion.5
  221.3 1.4 fusion.42
  225.6 1.4 convert_bitcast_fusion.5
  227.9 1.4 fusion.42
  232.2 1.4 convert_bitcast_fusion.5
  234.5 1.4 fusion.42
  238.7 1.4 convert_bitcast_fusion.5
  241.0 1.4 fusion.42
  245.3 1.4 convert_bitcast_fusion.5
  247.6 1.4 fusion.42
  251.9 1.4 convert_bitcast_fusion.5
  254.2 1.4 fusion.42
  258.4 1.4 convert_bitcast_fusion.5
  260.7 1.4 fusion.42
  265.0 1.4 convert_bitcast_fusion.5
  267.3 1.4 fusion.42
  271.6 1.4 convert_bitcast_fusion.5
  273.9 1.4 fusion.42
  278.2 1.4 convert_bitcast_fusion.5
  280.4 1.4 fusion.42
  284.7 1.4 convert_bitcast_fusion.5
  287.0 1.4 fusion.42
  291.3 1.4 convert_bitcast_fusion.5
  293.6 1.4 fusion.42
  297.9 1.4 convert_bitcast_fusion.5
  300.2 1.4 fusion.42
  304.4 1.4 convert_bitcast_fusion.5
  306.7 1.4 fusion.42
  308.8 1.7 copy-done
  (137 shorter events, 64.1 us)
Async XLA Ops:
  0.6 1.9 copy-start.7
  106.5 6.5 %copy-start.8 = (f32[64,512]{1,0:T(8,128)S(1)}, f32[64,512]{1,0:T(8,128)}, u32[]{:S(2)}) copy-start(f32[64,512]{1,0:T(8,128)} %param.11) | copy-start | bytes 393220
  106.5 41.0 %all-to-all-start.1 = ((bf16[4,2,196608]{2,1,0:T(2,128)(2,1)}), bf16[4,2,196608]{2,1,0:T(2,128)(2,1)S(1)}, u32[]{:S(2)}, u32[]{:S(2)}) async-start(bf16[4,2,196608]{2,1,0:T(2,128)(2,1)} %reshape.109), calls=%async_computation.1 | async-start | bytes 6291456 | tf_op jit(solution)/shard_map/all_to_all | solution.py:103
  115.1 0.7 copy-start.4
  165.7 9.2 %collective-permute-start.1 = (bf16[16,3,64,4]{2,0,3,1:T(8,128)(2,1)S(1)}, bf16[16,3,64,4]{2,0,3,1:T(8,128)(2,1)S(1)}, u32[]{:S(2)}, u32[]{:S(2)}) collective-permute-start(bf16[16,3,64,4]{2,0,3,1:T(8,128)(2,1)S(1)} %copy.47), channel_id=1, source_target_pairs={{32,0},{64,32},{96,64},{33,1},{65,33},{97,65},{34,2},{66,34},{98,6... | collective-permute-start | bytes 73736 | tf_op jit(solution)/shard_map/ppermute | solution.py:19
  168.8 4.8 %collective-permute-start = (bf16[16,3,64,4]{2,0,3,1:T(8,128)(2,1)S(1)}, bf16[16,3,64,4]{2,0,3,1:T(8,128)(2,1)S(1)}, u32[]{:S(2)}, u32[]{:S(2)}) collective-permute-start(bf16[16,3,64,4]{2,0,3,1:T(8,128)(2,1)S(1)} %copy.46), channel_id=1, source_target_pairs={{0,32},{32,64},{64,96},{1,33},{33,65},{65,97},{2,34},{34,66},{66,9... | collective-permute-start | bytes 73736 | tf_op jit(solution)/shard_map/ppermute | solution.py:18
  176.1 16.4 %copy-start.5 = (bf16[16,3,64,4]{3,2,1,0:T(8,128)(2,1)S(1)}, bf16[16,3,64,4]{3,2,1,0:T(8,128)(2,1)}, u32[]{:S(2)}) copy-start(bf16[16,3,64,4]{3,2,1,0:T(8,128)(2,1)} %copy.48) | copy-start | bytes 73732
  176.1 16.4 %copy-start.6 = (bf16[16,3,64,4]{3,2,1,0:T(8,128)(2,1)S(1)}, bf16[16,3,64,4]{3,2,1,0:T(8,128)(2,1)}, u32[]{:S(2)}) copy-start(bf16[16,3,64,4]{3,2,1,0:T(8,128)(2,1)} %copy.49) | copy-start | bytes 73732
  177.9 8.8 %collective-permute-start.2 = (bf16[16,3,4,520]{3,2,1,0:T(4,128)(2,1)S(1)}, bf16[16,3,4,520]{3,2,1,0:T(4,128)(2,1)S(1)}, u32[]{:S(2)}, u32[]{:S(2)}) collective-permute-start(bf16[16,3,4,520]{3,2,1,0:T(4,128)(2,1)S(1)} %get-tuple-element.126), channel_id=1, source_target_pairs={{0,1},{1,2},{2,3},{3,4},{4,5},{5,6},{6,7},{7,8},{8,9},{9,10},{10,1... | collective-permute-start | bytes 599048 | tf_op jit(solution)/shard_map/ppermute | solution.py:18
  183.6 8.9 %collective-permute-start.3 = (bf16[16,3,4,520]{3,2,1,0:T(4,128)(2,1)S(1)}, bf16[16,3,4,520]{3,2,1,0:T(4,128)(2,1)S(1)}, u32[]{:S(2)}, u32[]{:S(2)}) collective-permute-start(bf16[16,3,4,520]{3,2,1,0:T(4,128)(2,1)S(1)} %get-tuple-element.127), channel_id=1, source_target_pairs={{1,0},{2,1},{3,2},{4,3},{5,4},{6,5},{7,6},{8,7},{9,8},{10,9},{11,1... | collective-permute-start | bytes 599048 | tf_op jit(solution)/shard_map/ppermute | solution.py:19
  200.2 3.5 %copy-start.1 = (f32[3,8,64,512]{3,2,1,0:T(8,128)S(1)}, f32[3,8,64,512]{3,2,1,0:T(8,128)}, u32[]{:S(2)}) copy-start(f32[3,8,64,512]{3,2,1,0:T(8,128)} %param.15) | copy-start | bytes 9437188
  200.2 3.5 %copy-start.2 = (f32[3,64,512]{2,1,0:T(8,128)S(1)}, f32[3,64,512]{2,1,0:T(8,128)}, u32[]{:S(2)}) copy-start(f32[3,64,512]{2,1,0:T(8,128)} %param.14) | copy-start | bytes 1179652
  207.3 0.9 copy-start.3
  213.8 0.9 copy-start.3
  220.4 0.9 copy-start.3
  227.0 0.9 copy-start.3
  233.6 0.9 copy-start.3
  240.1 0.9 copy-start.3
  246.7 0.9 copy-start.3
  253.3 0.9 copy-start.3
  259.8 0.9 copy-start.3
  266.4 0.9 copy-start.3
  273.0 0.9 copy-start.3
  279.5 0.9 copy-start.3
  286.1 0.9 copy-start.3
  292.7 0.9 copy-start.3
  299.3 0.9 copy-start.3
  305.8 0.9 copy-start.3
  308.8 1.7 copy-start
where the time goes:
time: 313 us; the launch traced here: 310 us
  local copies, waits for them, and re-layouts  105 us (34%)
  other arithmetic  97.3 us (31%)
  blocking collectives  43.9 us (14%)
  waiting for transfers between devices  39.8 us (13%)
  starting transfers between devices  16.1 us (5%)
  matrix products  6.73 us (2%)
    unnamed x22, local copies, waits for them, and re-layouts  48.3 us
    all_to_all x1, blocking collectives, body(): lax.all_to_all(flipped, 'tile', split_axis=2, concat_axis=3, tiled=True)  43.9 us
    all_to_all x1, waiting for transfers between devices, body(): lax.all_to_all(lax.all_to_all(flipped, 'tile', split_axis=2, concat_axis=...  30.1 us
    another operation x16, other arithmetic, velocity_of(): jnp.stack([mean_inflow + first_diag * state[0], second_low * state[0] + s...  22.1 us
    add x16, other arithmetic, march(): return (1.0 - courant) * current + courant * upstream  22.1 us
    all_to_all x2, local copies, waits for them, and re-layouts, body(): lax.all_to_all(flipped, 'tile', split_axis=2, concat_axis=3, tiled=True)  21.3 us
    add x16, other arithmetic, advance(): state = decay * state + gain * plane  20.4 us
    sub x16, other arithmetic, march(): return (1.0 - courant) * current + courant * upstream  14.6 us
  transfers between devices with their start and end apart: 5, of which 4 were waited for; matrix products, arithmetic and copies ran while one was open for 2% of the time, Pallas kernels for 0%

commit v1 on v0

--- a/solution.py
+++ b/solution.py
@@ -6,6 +6,29 @@
 
 LS = 2
 FW = 4
+
+
+def split_up(value, dim, peers):
+    dims = value.shape
+    blocks = value.reshape(*dims[:dim], peers, dims[dim] // peers, *dims[dim + 1 :])
+    return jnp.moveaxis(blocks, dim, 0)
+
+
+def laid_out(parts, dim):
+    dims = list(parts.shape[1:])
+    dims[dim] *= parts.shape[0]
+    return jnp.moveaxis(parts, 0, dim).reshape(dims)
+
+
+def rotated_exchange(x, axis, split_dim, concat_dim):
+    size, position = (lax.axis_size(axis), lax.axis_index(axis))
+    parts = split_up(x, split_dim, size)
+    outs = [parts[position]]
+    for step in range(1, size):
+        sent = parts[(position + step) % size]
+        outs.append(lax.ppermute(sent, axis, [(i, (i + step) % size) for i in range(size)]))
+    parts = jnp.stack(outs)[(position - jnp.arange(size)) % size]
+    return laid_out(parts, concat_dim)
 
 
 def padded_2(value, sides, width, wrap):
@@ -100,12 +123,8 @@
 def body(noise, stress, timescale, mean_inflow, courant, prior_state, field):
     taps = filter_taps()
     flipped = jnp.swapaxes(noise, 2, 3)
-    tiles = lax.all_to_all(
-        lax.all_to_all(flipped, "tile", split_axis=2, concat_axis=3, tiled=True),
-        "grp",
-        split_axis=3,
-        concat_axis=0,
-        tiled=True,
+    tiles = rotated_exchange(
+        lax.all_to_all(flipped, "tile", split_axis=2, concat_axis=3, tiled=True), "grp", 3, 0
     )
     banded = padded_2(tiles, (("grp", 3),), FW, False)
     widened = padded_2(banded, (("tile", 2),), FW, True)

time: 313 us -> 296 us (0.946)
  blocking collectives: 43.9 us -> 0 us
  waiting for transfers between devices: 39.8 us -> 75 us
  local copies, waits for them, and re-layouts: 105 us -> 89.3 us
  starting transfers between devices: 16.1 us -> 23.7 us
    all_to_all x1 -> x0, blocking collectives: 43.9 us -> none  [body(): lax.all_to_all(flipped, 'tile', split_axis=2, concat_axis=3, tiled=True)]
    ppermute x0 -> x3, waiting for transfers between devices: none -> 31.2 us  [rotated_exchange(): lax.ppermute(sent, axis, [(i, (i + step) % size) for i in range(size)])]
    unnamed x22 -> x26, local copies, waits for them, and re-layouts: 48.3 us -> 35 us
    all_to_all x2 -> x1, local copies, waits for them, and re-layouts: 21.3 us -> 9.46 us  [body(): lax.all_to_all(flipped, 'tile', split_axis=2, concat_axis=3, tiled=True)]
    reshape x0 -> x1, local copies, waits for them, and re-layouts: none -> 8.47 us  [split_up(): value.reshape(*dims[:dim], peers, dims[dim] // peers, *dims[dim + 1:])]
    all_to_all x1 -> x0, local copies, waits for them, and re-layouts: 8.27 us -> none  [body(): lax.all_to_all(lax.all_to_all(flipped, 'tile', split_axis=2, concat_axis=...]
    another operation x0 -> x1, local copies, waits for them, and re-layouts: none -> 7.01 us
    all_to_all x1, waiting for transfers between devices: 30.1 us -> 35 us  [body(): lax.all_to_all(flipped, 'tile', split_axis=2, concat_axis=3, tiled=True)]
  transfers between devices with their start and end apart: 5 -> 8, of which waited for: 4 -> 7; matrix products, arithmetic and copies ran while one was open for 2% -> 2% of each run, Pallas kernels for 0% -> 0%
where the time goes in v1:
time: 296 us; the launch traced here: 294 us
  other arithmetic  97.1 us (33%)
  local copies, waits for them, and re-layouts  89.3 us (30%)
  waiting for transfers between devices  75 us (25%)
  starting transfers between devices  23.7 us (8%)
  matrix products  6.74 us (2%)
    all_to_all x1, waiting for transfers between devices, body(): lax.all_to_all(flipped, 'tile', split_axis=2, concat_axis=3, tiled=True)  35 us
    unnamed x26, local copies, waits for them, and re-layouts  35 us
    ppermute x3, waiting for transfers between devices, rotated_exchange(): lax.ppermute(sent, axis, [(i, (i + step) % size) for i in range(size)])  31.2 us
    another operation x16, other arithmetic, velocity_of(): jnp.stack([mean_inflow + first_diag * state[0], second_low * state[0] + s...  22.1 us
    add x16, other arithmetic, march(): return (1.0 - courant) * current + courant * upstream  22.1 us
    add x16, other arithmetic, advance(): state = decay * state + gain * plane  20.4 us
    sub x16, other arithmetic, march(): return (1.0 - courant) * current + courant * upstream  14.6 us
    dynamic_update_slice x16, other arithmetic, tile_chain(): (state, result), inflow = lax.scan(advance, (prior_state, field), filtered)  11.1 us
  transfers between devices with their start and end apart: 8, of which 7 were waited for; matrix products, arithmetic and copies ran while one was open for 2% of the time, Pallas kernels for 0%

profile of v1, /device:TPU:63, one launch (start us, length us, event | category | flops | bytes accessed | tf_op | source)
XLA Modules:
  0.0 294.0 jit_solution(15087510102781746538)
XLA Ops:
  0.6 1.9 copy-done.7
  2.5 7.2 %copy.34 = bf16[4,3,64,2048]{2,0,1,3:T(4,128)(2,1)} copy(bf16[4,3,64,2048]{3,2,1,0:T(8,128)(2,1)S(1)} %copy-done.7) | data formatting | bytes 6291456 | tf_op args[0]
  9.7 7.7 %bitcast_bitcast_fusion = bf16[2048,3,4,64]{3,2,1,0:T(4,128)(2,1)} fusion(bf16[4,3,64,2048]{2,0,1,3:T(4,128)(2,1)} %copy.34), kind=kLoop, calls=%fused_computation.90 | loop fusion | bytes 6291456
  17.4 8.7 %reshape.180 = bf16[32,2,24576]{2,1,0:T(2,128)(2,1)} reshape(bf16[2048,3,4,64]{3,2,1,0:T(4,128)(2,1)} %bitcast_bitcast_fusion) | data formatting | bytes 6291456
  26.2 7.6 %all-to-all-start = ((bf16[32,2,24576]{2,1,0:T(2,128)(2,1)}), bf16[32,2,24576]{2,1,0:T(2,128)(2,1)S(1)}, u32[]{:S(2)}, u32[]{:S(2)}) async-start(bf16[32,2,24576]{2,1,0:T(2,128)(2,1)} %reshape.180), calls=%async_computation | async-start | bytes 6291456 | tf_op jit(solution)/shard_map/all_to_all | solution.py:127
  35.2 35.0 %all-to-all-done = bf16[32,2,24576]{2,1,0:T(2,128)(2,1)S(1)} async-done(((bf16[32,2,24576]{2,1,0:T(2,128)(2,1)}), bf16[32,2,24576]{2,1,0:T(2,128)(2,1)S(1)}, u32[]{:S(2)}, u32[]{:S(2)}) %all-to-all-start) | async-done | bytes 3145760 | tf_op jit(solution)/shard_map/all_to_all | solution.py:127
  70.3 6.2 %reshape.181 = bf16[2048,3,4,64]{3,2,1,0:T(4,128)(2,1)} reshape(bf16[32,2,24576]{2,1,0:T(2,128)(2,1)S(1)} %all-to-all-done) | data formatting | bytes 6291456
  76.4 9.5 %copy.60 = bf16[4,3,32,64,64]{4,2,3,1,0:T(8,128)(2,1)} copy(bf16[4,3,32,64,64]{4,0,1,3,2:T(4,128)(2,1)} %bitcast.139) | data formatting | bytes 6291456 | tf_op jit(solution)/shard_map/all_to_all | solution.py:127
  85.9 8.5 %reshape.167 = bf16[4,3,64,4,512]{4,3,2,1,0:T(4,128)(2,1)S(1)} reshape(bf16[4,3,64,32,64]{4,3,2,1,0:T(8,128)(2,1)} %bitcast.140) | data formatting | bytes 6291456 | tf_op jit(solution)/shard_map/reshape | solution.py:13
  94.4 7.0 %constant_dynamic-slice_fusion.3 = (bf16[4,3,64,1,512]{4,3,2,1,0:T(2,128)(2,1)S(1)}, bf16[4,3,64,1,512]{4,3,2,1,0:T(2,128)(2,1)S(1)}, bf16[4,3,64,1,512]{4,3,2,1,0:T(2,128)(2,1)S(1)}, bf16[4,3,64,1,512]{4,3,2,1,0:T(2,128)(2,1)S(1)}) fusion(bf16[4,3,64,4,512]{4,3,2,1,0:T(4,128)(2,1)S(1)} %reshape.167, s32[]{:T(128)S(6)} %select_n.58, s32[]{:T(128)S(6)} %select_n.64, ...), kind=kLoop, calls=%fused_computation.80 | loop fusion | bytes 6291472 | tf_op jit(solution)/shard_map/dynamic-slice
  102.1 1.7 collective-permute-start
  105.0 2.0 collective-permute-start.2
  109.7 10.6 %collective-permute-done = bf16[4,3,64,512]{3,2,1,0:T(8,128)(2,1)S(1)} collective-permute-done((bf16[4,3,64,512]{3,2,1,0:T(8,128)(2,1)S(1)}, bf16[4,3,64,512]{3,2,1,0:T(8,128)(2,1)S(1)}, u32[]{:S(2)}, u32[]{:S(2)}) %collective-permute-start) | collective-permute-done | bytes 786464 | tf_op jit(solution)/shard_map/ppermute | solution.py:29
  120.3 2.9 %collective-permute-done.1 = bf16[4,3,64,512]{3,2,1,0:T(8,128)(2,1)S(1)} collective-permute-done((bf16[4,3,64,512]{3,2,1,0:T(8,128)(2,1)S(1)}, bf16[4,3,64,512]{3,2,1,0:T(8,128)(2,1)S(1)}, u32[]{:S(2)}, u32[]{:S(2)}) %collective-permute-start.1) | collective-permute-done | bytes 786464 | tf_op jit(solution)/shard_map/ppermute | solution.py:29
  123.2 17.7 %collective-permute-done.2 = bf16[4,3,64,512]{3,2,1,0:T(8,128)(2,1)S(1)} collective-permute-done((bf16[4,3,64,512]{3,2,1,0:T(8,128)(2,1)S(1)}, bf16[4,3,64,512]{3,2,1,0:T(8,128)(2,1)S(1)}, u32[]{:S(2)}, u32[]{:S(2)}) %collective-permute-start.2) | collective-permute-done | bytes 786464 | tf_op jit(solution)/shard_map/ppermute | solution.py:29
  140.9 1.9 pad_maximum_fusion.1
  142.8 2.6 gather_fusion
  145.4 1.5 fusion.40
  147.0 1.5 copy.36
  148.5 1.5 copy.37
  150.0 1.9 collective-permute-start.4
  151.9 3.4 %collective-permute-start.3 = (bf16[16,3,64,4]{2,0,3,1:T(8,128)(2,1)S(1)}, bf16[16,3,64,4]{2,0,3,1:T(8,128)(2,1)S(1)}, u32[]{:S(2)}, u32[]{:S(2)}) collective-permute-start(bf16[16,3,64,4]{2,0,3,1:T(8,128)(2,1)S(1)} %copy.36), channel_id=1, source_target_pairs={{0,32},{32,64},{64,96},{1,33},{33,65},{65,97},{2,34},{34,66},{66,9... | collective-permute-start | bytes 73736 | tf_op jit(solution)/shard_map/ppermute | solution.py:41
  159.3 1.8 pad_maximum_fusion.4
  161.1 6.0 %collective-permute-start.5 = (bf16[16,3,4,520]{3,2,1,0:T(4,128)(2,1)S(1)}, bf16[16,3,4,520]{3,2,1,0:T(4,128)(2,1)S(1)}, u32[]{:S(2)}, u32[]{:S(2)}) collective-permute-start(bf16[16,3,4,520]{3,2,1,0:T(4,128)(2,1)S(1)} %get-tuple-element.126), channel_id=1, source_target_pairs={{0,1},{1,2},{2,3},{3,4},{4,5},{5,6},{6,7},{7,8},{8,9},{9,10},{10,1... | collective-permute-start | bytes 599048 | tf_op jit(solution)/shard_map/ppermute | solution.py:41
  167.1 1.6 sqrt_bitcast_fusion
  168.7 1.6 collective-permute-done.5
  170.3 5.8 %collective-permute-done.6 = bf16[16,3,4,520]{3,2,1,0:T(4,128)(2,1)S(1)} collective-permute-done((bf16[16,3,4,520]{3,2,1,0:T(4,128)(2,1)S(1)}, bf16[16,3,4,520]{3,2,1,0:T(4,128)(2,1)S(1)}, u32[]{:S(2)}, u32[]{:S(2)}) %collective-permute-start.6) | collective-permute-done | bytes 199712 | tf_op jit(solution)/shard_map/ppermute | solution.py:42
  176.1 4.2 %convert_bitcast_fusion.3 = bf16[16,3,64,520]{3,2,1,0:T(8,128)(2,1)S(1)} fusion(bf16[16,3,4,520]{3,2,1,0:T(4,128)(2,1)S(1)} %collective-permute-done.6, bf16[16,3,64,4]{3,2,1,0:T(8,128)(2,1)S(1)} %copy-done.6, bf16[16,3,64,512]{3,2,1,0:T(8,128)(2,1)S(1)} %bitcast.143, bf16[16,3,64,4]{3,2,1,0:T(8,128)(2,1)S(1)} %copy-done.5, ...), kind=kOutput, calls=%fused_computation.36 | convolution fusion | flops 249600000 | bytes 6798336 | tf_op jit(solution)/shard_map/ij,pcjz->pciz/dot_general | solution.py:79
  181.2 2.6 fusion.18
  183.8 3.5 %copy.59 = f32[16,3,4,8,8,128]{5,4,2,3,1,0:T(8,128)} copy(f32[16,3,4,8,8,128]{5,4,3,2,1,0:T(8,128)S(1)} %fusion.18) | data formatting | bytes 12582912 | tf_op jit(solution)/shard_map/reshape | solution.py:73
  187.2 105.1 %while.14 = (s32[]{:T(128)}, f32[3,64,512]{2,1,0:T(8,128)S(1)}, f32[3,8,64,512]{3,2,1,0:T(8,128)S(1)}, bf16[16,3,64,512]{3,2,1,0:T(8,128)(2,1)}, f32[64,512]{1,0...) while((s32[]{:T(128)}, f32[3,64,512]{2,1,0:T(8,128)S(1)}, ...), condition=%wide.region_4.5_spmd, body=%wide.region_3.4_spmd.sunk | while | flops 4685826 | bytes 20512960 | solution.py:119
  189.4 1.4 convert_bitcast_fusion.5
  191.7 1.4 fusion.44
  196.0 1.4 convert_bitcast_fusion.5
  198.3 1.4 fusion.44
  202.6 1.4 convert_bitcast_fusion.5
  204.9 1.4 fusion.44
  209.2 1.4 convert_bitcast_fusion.5
  211.4 1.4 fusion.44
  215.7 1.4 convert_bitcast_fusion.5
  218.0 1.4 fusion.44
  222.3 1.4 convert_bitcast_fusion.5
  224.6 1.4 fusion.44
  228.9 1.4 convert_bitcast_fusion.5
  231.2 1.4 fusion.44
  235.4 1.4 convert_bitcast_fusion.5
  237.7 1.4 fusion.44
  242.0 1.4 convert_bitcast_fusion.5
  244.3 1.4 fusion.44
  248.6 1.4 convert_bitcast_fusion.5
  250.9 1.4 fusion.44
  255.1 1.4 convert_bitcast_fusion.5
  257.4 1.4 fusion.44
  261.7 1.4 convert_bitcast_fusion.5
  264.0 1.4 fusion.44
  268.3 1.4 convert_bitcast_fusion.5
  270.6 1.4 fusion.44
  274.9 1.4 convert_bitcast_fusion.5
  277.1 1.4 fusion.44
  281.4 1.4 convert_bitcast_fusion.5
  283.7 1.4 fusion.44
  288.0 1.4 convert_bitcast_fusion.5
  290.3 1.4 fusion.44
  292.4 1.7 copy-done
  (150 shorter events, 70.4 us)
Async XLA Ops:
  0.6 1.9 copy-start.7
  26.2 44.1 %all-to-all-start = ((bf16[32,2,24576]{2,1,0:T(2,128)(2,1)}), bf16[32,2,24576]{2,1,0:T(2,128)(2,1)S(1)}, u32[]{:S(2)}, u32[]{:S(2)}) async-start(bf16[32,2,24576]{2,1,0:T(2,128)(2,1)} %reshape.180), calls=%async_computation | async-start | bytes 6291456 | tf_op jit(solution)/shard_map/all_to_all | solution.py:127
  101.4 5.7 %copy-start.8 = (f32[6,64,512]{2,1,0:T(8,128)S(1)}, f32[6,64,512]{2,1,0:T(8,128)}, u32[]{:S(2)}) copy-start(f32[6,64,512]{2,1,0:T(8,128)} %param.10) | copy-start | bytes 2359300
  101.4 5.7 %copy-start.9 = (f32[64,512]{1,0:T(8,128)S(1)}, f32[64,512]{1,0:T(8,128)}, u32[]{:S(2)}) copy-start(f32[64,512]{1,0:T(8,128)} %param.11) | copy-start | bytes 393220
  102.1 18.2 %collective-permute-start = (bf16[4,3,64,512]{3,2,1,0:T(8,128)(2,1)S(1)}, bf16[4,3,64,512]{3,2,1,0:T(8,128)(2,1)S(1)}, u32[]{:S(2)}, u32[]{:S(2)}) collective-permute-start(bf16[4,3,64,512]{3,2,1,0:T(8,128)(2,1)S(1)} %bitcast.151), channel_id=1, source_target_pairs={{0,32},{32,64},{64,96},{96,0},{1,33},{33,65},{65,97},{97,1},{2,34}... | collective-permute-start | bytes 2359304 | tf_op jit(solution)/shard_map/ppermute | solution.py:29
  103.8 19.4 %collective-permute-start.1 = (bf16[4,3,64,512]{3,2,1,0:T(8,128)(2,1)S(1)}, bf16[4,3,64,512]{3,2,1,0:T(8,128)(2,1)S(1)}, u32[]{:S(2)}, u32[]{:S(2)}) collective-permute-start(bf16[4,3,64,512]{3,2,1,0:T(8,128)(2,1)S(1)} %bitcast.150), channel_id=1, source_target_pairs={{0,64},{32,96},{64,0},{96,32},{1,65},{33,97},{65,1},{97,33},{2,66}... | collective-permute-start | bytes 2359304 | tf_op jit(solution)/shard_map/ppermute | solution.py:29
  105.0 36.0 %collective-permute-start.2 = (bf16[4,3,64,512]{3,2,1,0:T(8,128)(2,1)S(1)}, bf16[4,3,64,512]{3,2,1,0:T(8,128)(2,1)S(1)}, u32[]{:S(2)}, u32[]{:S(2)}) collective-permute-start(bf16[4,3,64,512]{3,2,1,0:T(8,128)(2,1)S(1)} %bitcast.149), channel_id=1, source_target_pairs={{0,96},{32,0},{64,32},{96,64},{1,97},{33,1},{65,33},{97,65},{2,98}... | collective-permute-start | bytes 2359304 | tf_op jit(solution)/shard_map/ppermute | solution.py:29
  108.1 0.7 copy-start.4
  150.0 8.0 %collective-permute-start.4 = (bf16[16,3,64,4]{2,0,3,1:T(8,128)(2,1)S(1)}, bf16[16,3,64,4]{2,0,3,1:T(8,128)(2,1)S(1)}, u32[]{:S(2)}, u32[]{:S(2)}) collective-permute-start(bf16[16,3,64,4]{2,0,3,1:T(8,128)(2,1)S(1)} %copy.37), channel_id=1, source_target_pairs={{32,0},{64,32},{96,64},{33,1},{65,33},{97,65},{34,2},{66,34},{98,6... | collective-permute-start | bytes 73736 | tf_op jit(solution)/shard_map/ppermute | solution.py:42
  151.9 4.8 %collective-permute-start.3 = (bf16[16,3,64,4]{2,0,3,1:T(8,128)(2,1)S(1)}, bf16[16,3,64,4]{2,0,3,1:T(8,128)(2,1)S(1)}, u32[]{:S(2)}, u32[]{:S(2)}) collective-permute-start(bf16[16,3,64,4]{2,0,3,1:T(8,128)(2,1)S(1)} %copy.36), channel_id=1, source_target_pairs={{0,32},{32,64},{64,96},{1,33},{33,65},{65,97},{2,34},{34,66},{66,9... | collective-permute-start | bytes 73736 | tf_op jit(solution)/shard_map/ppermute | solution.py:41
  159.3 16.8 %copy-start.5 = (bf16[16,3,64,4]{3,2,1,0:T(8,128)(2,1)S(1)}, bf16[16,3,64,4]{3,2,1,0:T(8,128)(2,1)}, u32[]{:S(2)}) copy-start(bf16[16,3,64,4]{3,2,1,0:T(8,128)(2,1)} %copy.38) | copy-start | bytes 73732
  159.3 16.8 %copy-start.6 = (bf16[16,3,64,4]{3,2,1,0:T(8,128)(2,1)S(1)}, bf16[16,3,64,4]{3,2,1,0:T(8,128)(2,1)}, u32[]{:S(2)}) copy-start(bf16[16,3,64,4]{3,2,1,0:T(8,128)(2,1)} %copy.39) | copy-start | bytes 73732
  161.1 9.2 %collective-permute-start.5 = (bf16[16,3,4,520]{3,2,1,0:T(4,128)(2,1)S(1)}, bf16[16,3,4,520]{3,2,1,0:T(4,128)(2,1)S(1)}, u32[]{:S(2)}, u32[]{:S(2)}) collective-permute-start(bf16[16,3,4,520]{3,2,1,0:T(4,128)(2,1)S(1)} %get-tuple-element.126), channel_id=1, source_target_pairs={{0,1},{1,2},{2,3},{3,4},{4,5},{5,6},{6,7},{7,8},{8,9},{9,10},{10,1... | collective-permute-start | bytes 599048 | tf_op jit(solution)/shard_map/ppermute | solution.py:41
  167.1 8.9 %collective-permute-start.6 = (bf16[16,3,4,520]{3,2,1,0:T(4,128)(2,1)S(1)}, bf16[16,3,4,520]{3,2,1,0:T(4,128)(2,1)S(1)}, u32[]{:S(2)}, u32[]{:S(2)}) collective-permute-start(bf16[16,3,4,520]{3,2,1,0:T(4,128)(2,1)S(1)} %get-tuple-element.127), channel_id=1, source_target_pairs={{1,0},{2,1},{3,2},{4,3},{5,4},{6,5},{7,6},{8,7},{9,8},{10,9},{11,1... | collective-permute-start | bytes 599048 | tf_op jit(solution)/shard_map/ppermute | solution.py:42
  183.7 3.5 %copy-start.1 = (f32[3,8,64,512]{3,2,1,0:T(8,128)S(1)}, f32[3,8,64,512]{3,2,1,0:T(8,128)}, u32[]{:S(2)}) copy-start(f32[3,8,64,512]{3,2,1,0:T(8,128)} %param.15) | copy-start | bytes 9437188
  183.8 3.5 %copy-start.2 = (f32[3,64,512]{2,1,0:T(8,128)S(1)}, f32[3,64,512]{2,1,0:T(8,128)}, u32[]{:S(2)}) copy-start(f32[3,64,512]{2,1,0:T(8,128)} %param.14) | copy-start | bytes 1179652
  190.8 0.9 copy-start.3
  197.4 0.9 copy-start.3
  204.0 0.9 copy-start.3
  210.5 0.9 copy-start.3
  217.1 0.9 copy-start.3
  223.7 0.9 copy-start.3
  230.2 0.9 copy-start.3
  236.8 0.9 copy-start.3
  243.4 0.9 copy-start.3
  250.0 0.9 copy-start.3
  256.5 0.9 copy-start.3
  263.1 0.9 copy-start.3
  269.7 0.9 copy-start.3
  276.2 0.9 copy-start.3
  282.8 0.9 copy-start.3
  289.4 0.9 copy-start.3
  292.4 1.7 copy-start
